TPU v7x, 128 devices: a whole 4x4x4 slice. The times are simulated.
128 devices in a mesh: section: 8 (over y, core), dp: 16 (over z, x).
Axes of the slice: x: 4, y: 4, z: 4, core: 2. Of those that a mesh axis runs over, the one named last changes fastest.
Arguments:
- acts: bfloat16 [8, 8192, 3584], P('section', 'dp'), may hold values from -400 to 400
- cotangent: bfloat16 [8192, 3584], P('dp'), may hold values from -6 to 6
- frozen: bfloat16 [8, 3584, 3584], P('section', 'dp'), may hold values from -0.09375 to 0.09375
- down_adapter: bfloat16 [8, 16, 3584], P('section'), may hold values from -0.25 to 0.25
- up_adapter: bfloat16 [8, 16, 3584], P('section'), may hold values from -0.25 to 0.25
- example_ids: int32 [16, 4], P('dp'), may hold values from 0 to 3, each once within a row
- lengths: int32 [16, 4], P('dp'), may hold values from 32 to 128
Outputs:
- grad_down: float32 [8, 16, 3584], P('section', None, 'dp')
- grad_up: float32 [8, 16, 3584], P('section', None, 'dp')
- example_norms: float32 [16, 4], P('dp')
Inputs may be any that keep to these rules, and one draw needn't show every extreme that they name: `example_ids`: each row is an ordering of the 4 examples of one replica.
All inputs are finite; a program needn't handle non-finite values.
Results may differ from a plain program's by a relative error of at most 0.009.
Values may be sent and summed in bfloat16 or wider, within the bound.
A program may use at most 128 MiB of HBM per device.

v0:
```python
import math
import jax
import jax.numpy as jnp
from jax import lax
from jax.sharding import PartitionSpec as P


def from_behind(value, axis, steps):
    count = lax.axis_size(axis)
    first, last = (max(0, -steps), min(count, count - steps))
    return lax.ppermute(value, axis, [(source, source + steps) for source in range(first, last)])


def sent_to_all(value, axis):
    size = lax.axis_size(axis)
    return lax.all_to_all(
        jnp.broadcast_to(value[None], (size, *value.shape)), axis, 0, 0, tiled=True
    )


def taken_together(value, axis):
    return sent_to_all(value, axis).sum(axis=0)


def split_up(value, dim, size):
    shape = value.shape
    pieces = value.reshape(*shape[:dim], size, shape[dim] // size, *shape[dim + 1 :])
    return jnp.moveaxis(pieces, dim, 0)


def sent_and_summed(value, axis, dim):
    pieces = split_up(value, dim, lax.axis_size(axis))
    arrived = lax.all_to_all(pieces, axis, split_axis=0, concat_axis=0, tiled=True)
    return arrived.sum(axis=0)


def side_by_side(arrays, axis, dim, along):
    ends, at = ([], 0)
    for a in arrays[:-1]:
        at += a.shape[along]
        ends.append(at)
    both = jnp.concatenate(arrays, axis=along)
    return tuple(jnp.split(sent_and_summed(both, axis, dim), ends, axis=along))


def on_device(acts, cotangent, frozen, down_adapter, up_adapter, example_ids, lengths):
    section_count = lax.axis_size("section")
    section_index = lax.axis_index("section")
    replica_count = lax.axis_size("dp")
    layer_inputs = acts[0]
    down_rows = down_adapter[0]
    up_rows = up_adapter[0]
    slot_count = example_ids.shape[1]
    positions = layer_inputs.shape[0] // slot_count
    features = layer_inputs.shape[1]
    rank_size = down_rows.shape[0]
    choose = (example_ids[0][:, None] == jnp.arange(slot_count, dtype=jnp.int32)[None, :]).astype(
        jnp.int32
    )
    slot_length = jnp.sum(choose * lengths[0][None, :], axis=1)
    live_mask = (jnp.arange(positions, dtype=jnp.int32)[None, :] < slot_length[:, None]).astype(
        jnp.bfloat16
    )
    seeded = cotangent.reshape(slot_count, positions, features) * live_mask[:, :, None]
    input_blocks = layer_inputs.reshape(slot_count, positions, features)
    clip_scale = math.sqrt(2.0 * rank_size * features) / math.sqrt(replica_count * slot_count)
    weight = lax.all_gather(frozen[0], "dp", axis=0, tiled=True)

    def backstep(out_grad):
        up_grad = jnp.dot(out_grad, up_rows.T, preferred_element_type=jnp.float32).astype(
            jnp.bfloat16
        )
        in_grad = jnp.dot(out_grad, weight.T, preferred_element_type=jnp.float32)
        in_grad = in_grad + jnp.dot(up_grad, down_rows, preferred_element_type=jnp.float32)
        return in_grad.astype(jnp.bfloat16)

    def local_terms(out_grad, inputs):
        up_grad = jnp.dot(out_grad, up_rows.T, preferred_element_type=jnp.float32).astype(
            jnp.bfloat16
        )
        down_act = jnp.dot(inputs, down_rows.T, preferred_element_type=jnp.float32).astype(
            jnp.bfloat16
        )
        down_term = jnp.dot(up_grad.T, inputs, preferred_element_type=jnp.float32)
        up_term = jnp.dot(down_act.T, out_grad, preferred_element_type=jnp.float32)
        square_sum = jnp.sum(down_term * down_term) + jnp.sum(up_term * up_term)
        return (square_sum, down_term, up_term)

    tick_count = slot_count + section_count - 1
    incoming = jnp.zeros((positions, features), jnp.bfloat16)
    stored_grads = jnp.zeros((slot_count, positions, features), jnp.bfloat16)
    sum_down = jnp.zeros((rank_size, features), jnp.float32)
    sum_up = jnp.zeros((rank_size, features), jnp.float32)
    slot_norms = jnp.zeros((slot_count,), jnp.float32)

    def tick_step(tick, carry):
        incoming, stored_grads, sum_down, sum_up, slot_norms = carry
        micro_index = tick - (section_count - 1 - section_index)
        active = (micro_index >= 0) & (micro_index < slot_count)
        held_index = jnp.clip(micro_index, 0, slot_count - 1)
        fresh = lax.dynamic_index_in_dim(seeded, held_index, 0, keepdims=False)
        start = jnp.where(section_index == section_count - 1, fresh, incoming)
        produced = lax.cond(active, backstep, lambda value: jnp.zeros_like(value), start)
        previous = lax.dynamic_index_in_dim(stored_grads, held_index, 0, keepdims=False)
        kept = jnp.where(active, start, previous)
        stored_grads = lax.dynamic_update_index_in_dim(stored_grads, kept, held_index, 0)
        incoming = from_behind(produced, "section", -1)
        return (incoming, stored_grads, sum_down, sum_up, slot_norms)

    carry = (incoming, stored_grads, sum_down, sum_up, slot_norms)
    incoming, stored_grads, sum_down, sum_up, slot_norms = lax.fori_loop(
        0, tick_count, tick_step, carry
    )
    square_sums, down_terms, up_terms = jax.vmap(local_terms)(stored_grads, input_blocks)
    totals = taken_together(square_sums, "section")
    slot_norms = jnp.sqrt(totals)
    factors = clip_scale / (slot_norms + 0.01)
    sum_down = jnp.sum(factors[:, None, None] * down_terms, axis=0)
    sum_up = jnp.sum(factors[:, None, None] * up_terms, axis=0)
    grad_down, grad_up = side_by_side((sum_down, sum_up), "dp", 1, 0)
    example_norms = jnp.sum(choose.astype(jnp.float32) * slot_norms[:, None], axis=0)
    return (grad_down[None], grad_up[None], example_norms[None])


def solution(mesh):
    in_specs = (
        P("section", "dp", None),
        P("dp", None),
        P("section", "dp", None),
        P("section", None, None),
        P("section", None, None),
        P("dp", None),
        P("dp", None),
    )
    out_specs = (P("section", None, "dp"), P("section", None, "dp"), P("dp", None))
    return jax.shard_map(
        on_device, mesh=mesh, in_specs=in_specs, out_specs=out_specs, check_vma=False
    )
```

profile of v0, /device:TPU:0, one launch (start us, length us, event | category | flops | bytes accessed | tf_op | source)
XLA Modules:
  0.0 538.0 jit_solution(118021196939126210)
XLA Ops:
  8.8 4.1 broadcast_multiply_fusion
  13.0 156.6 %all-gather.3.cloned.1.call-done = bf16[1,3584,3584]{2,1,0:T(8,128)(2,1)} async-done(((bf16[1,224,3584]{2,1,0:T(8,128)(2,1)}), bf16[1,3584,3584]{2,1,0:T(8,128)(2,1)}) %all-gather.3.cloned.1.call-update) | async-done | bytes 25690128 | tf_op jit(solution)/shard_map/all_gather | solution.py:67
  171.7 317.0 %while.17 = (s32[]{:T(128)}, bf16[128,3584]{1,0:T(8,128)(2,1)S(1)}, bf16[4,128,3584]{2,1,0:T(8,128)(2,1)}, s32[]{:T(128)}, pred[]{:T(512)}, /*index=5*/bf16[4,12...) while((s32[]{:T(128)}, bf16[128,3584]{1,0:T(8,128)(2,1)S(1)}, ...), condition=%wide.region_4.5_spmd, body=%wide.region_1.4_spmd.sunk | while | flops 3319531520 | bytes 42435348 | solution.py:111
  173.0 2.6 bitcast_dynamic-update-slice_fusion.2
  177.9 3.3 collective-permute-done
  182.4 2.6 bitcast_dynamic-update-slice_fusion.2
  187.4 13.0 %collective-permute-done = bf16[128,3584]{1,0:T(8,128)(2,1)S(1)} collective-permute-done((bf16[128,3584]{1,0:T(8,128)(2,1)}, bf16[128,3584]{1,0:T(8,128)(2,1)S(1)}, u32[]{:S(2)}, u32[]{:S(2)}) %collective-permute-start) | collective-permute-done | bytes 917536 | tf_op jit(solution)/shard_map/while/body/eval_jaxpr/ppermute | solution.py:11
  201.6 2.6 bitcast_dynamic-update-slice_fusion.2
  206.5 13.6 %collective-permute-done = bf16[128,3584]{1,0:T(8,128)(2,1)S(1)} collective-permute-done((bf16[128,3584]{1,0:T(8,128)(2,1)}, bf16[128,3584]{1,0:T(8,128)(2,1)S(1)}, u32[]{:S(2)}, u32[]{:S(2)}) %collective-permute-start) | collective-permute-done | bytes 917536 | tf_op jit(solution)/shard_map/while/body/eval_jaxpr/ppermute | solution.py:11
  226.3 13.6 %collective-permute-done = bf16[128,3584]{1,0:T(8,128)(2,1)S(1)} collective-permute-done((bf16[128,3584]{1,0:T(8,128)(2,1)}, bf16[128,3584]{1,0:T(8,128)(2,1)S(1)}, u32[]{:S(2)}, u32[]{:S(2)}) %collective-permute-start) | collective-permute-done | bytes 917536 | tf_op jit(solution)/shard_map/while/body/eval_jaxpr/ppermute | solution.py:11
  241.2 2.6 bitcast_dynamic-update-slice_fusion.2
  246.1 13.6 %collective-permute-done = bf16[128,3584]{1,0:T(8,128)(2,1)S(1)} collective-permute-done((bf16[128,3584]{1,0:T(8,128)(2,1)}, bf16[128,3584]{1,0:T(8,128)(2,1)S(1)}, u32[]{:S(2)}, u32[]{:S(2)}) %collective-permute-start) | collective-permute-done | bytes 917536 | tf_op jit(solution)/shard_map/while/body/eval_jaxpr/ppermute | solution.py:11
  261.0 2.6 bitcast_dynamic-update-slice_fusion.2
  265.9 13.6 %collective-permute-done = bf16[128,3584]{1,0:T(8,128)(2,1)S(1)} collective-permute-done((bf16[128,3584]{1,0:T(8,128)(2,1)}, bf16[128,3584]{1,0:T(8,128)(2,1)S(1)}, u32[]{:S(2)}, u32[]{:S(2)}) %collective-permute-start) | collective-permute-done | bytes 917536 | tf_op jit(solution)/shard_map/while/body/eval_jaxpr/ppermute | solution.py:11
  285.7 78.1 %collective-permute-done = bf16[128,3584]{1,0:T(8,128)(2,1)S(1)} collective-permute-done((bf16[128,3584]{1,0:T(8,128)(2,1)}, bf16[128,3584]{1,0:T(8,128)(2,1)S(1)}, u32[]{:S(2)}, u32[]{:S(2)}) %collective-permute-start) | collective-permute-done | bytes 917536 | tf_op jit(solution)/shard_map/while/body/eval_jaxpr/ppermute | solution.py:11
  367.6 15.1 %conditional.2 = (bf16[128,3584]{1,0:T(8,128)(2,1)}) conditional(s32[]{:T(128)} %convert_element_type.57, () %tuple.55, (bf16[128,3584]{1,0:T(8,128)(2,1)S(1)}, bf16[3584,3584]{1,0:T(8,128)(2,1)}, bf16[16,3584]{1,0:T(8,128)(2,1)S(1)}, bf16[16,3584]{1,0:T(8,128)(2,1)S(1)}) %tuple.56), branch_computations={%region_2.2_spmd, %region_3.3_spmd} | conditional | flops 3318614016 | bytes 32342024 | solution.py:103
  367.6 12.9 %fusion.13 = f32[128,3584]{1,0:T(8,128)S(1)} fusion(bf16[128,3584]{1,0:T(8,128)(2,1)S(1)} %get-tuple-element.202, bf16[3584,3584]{1,0:T(8,128)(2,1)} %get-tuple-element.203), kind=kOutput, calls=%fused_computation.28 | convolution fusion | flops 3288334336 | bytes 28442624 | tf_op jit(solution)/shard_map/while/body/eval_jaxpr/cond/branch_1_fun/dot_general | solution.py:73
  384.0 13.6 %collective-permute-done = bf16[128,3584]{1,0:T(8,128)(2,1)S(1)} collective-permute-done((bf16[128,3584]{1,0:T(8,128)(2,1)}, bf16[128,3584]{1,0:T(8,128)(2,1)S(1)}, u32[]{:S(2)}, u32[]{:S(2)}) %collective-permute-start) | collective-permute-done | bytes 917536 | tf_op jit(solution)/shard_map/while/body/eval_jaxpr/ppermute | solution.py:11
  401.4 15.1 %conditional.2 = (bf16[128,3584]{1,0:T(8,128)(2,1)}) conditional(s32[]{:T(128)} %convert_element_type.57, () %tuple.55, (bf16[128,3584]{1,0:T(8,128)(2,1)S(1)}, bf16[3584,3584]{1,0:T(8,128)(2,1)}, bf16[16,3584]{1,0:T(8,128)(2,1)S(1)}, bf16[16,3584]{1,0:T(8,128)(2,1)S(1)}) %tuple.56), branch_computations={%region_2.2_spmd, %region_3.3_spmd} | conditional | flops 3318614016 | bytes 32342024 | solution.py:103
  401.4 12.9 %fusion.13 = f32[128,3584]{1,0:T(8,128)S(1)} fusion(bf16[128,3584]{1,0:T(8,128)(2,1)S(1)} %get-tuple-element.202, bf16[3584,3584]{1,0:T(8,128)(2,1)} %get-tuple-element.203), kind=kOutput, calls=%fused_computation.28 | convolution fusion | flops 3288334336 | bytes 28442624 | tf_op jit(solution)/shard_map/while/body/eval_jaxpr/cond/branch_1_fun/dot_general | solution.py:73
  417.8 13.6 %collective-permute-done = bf16[128,3584]{1,0:T(8,128)(2,1)S(1)} collective-permute-done((bf16[128,3584]{1,0:T(8,128)(2,1)}, bf16[128,3584]{1,0:T(8,128)(2,1)S(1)}, u32[]{:S(2)}, u32[]{:S(2)}) %collective-permute-start) | collective-permute-done | bytes 917536 | tf_op jit(solution)/shard_map/while/body/eval_jaxpr/ppermute | solution.py:11
  435.2 15.1 %conditional.2 = (bf16[128,3584]{1,0:T(8,128)(2,1)}) conditional(s32[]{:T(128)} %convert_element_type.57, () %tuple.55, (bf16[128,3584]{1,0:T(8,128)(2,1)S(1)}, bf16[3584,3584]{1,0:T(8,128)(2,1)}, bf16[16,3584]{1,0:T(8,128)(2,1)S(1)}, bf16[16,3584]{1,0:T(8,128)(2,1)S(1)}) %tuple.56), branch_computations={%region_2.2_spmd, %region_3.3_spmd} | conditional | flops 3318614016 | bytes 32342024 | solution.py:103
  435.2 12.9 %fusion.13 = f32[128,3584]{1,0:T(8,128)S(1)} fusion(bf16[128,3584]{1,0:T(8,128)(2,1)S(1)} %get-tuple-element.202, bf16[3584,3584]{1,0:T(8,128)(2,1)} %get-tuple-element.203), kind=kOutput, calls=%fused_computation.28 | convolution fusion | flops 3288334336 | bytes 28442624 | tf_op jit(solution)/shard_map/while/body/eval_jaxpr/cond/branch_1_fun/dot_general | solution.py:73
  451.6 13.6 %collective-permute-done = bf16[128,3584]{1,0:T(8,128)(2,1)S(1)} collective-permute-done((bf16[128,3584]{1,0:T(8,128)(2,1)}, bf16[128,3584]{1,0:T(8,128)(2,1)S(1)}, u32[]{:S(2)}, u32[]{:S(2)}) %collective-permute-start) | collective-permute-done | bytes 917536 | tf_op jit(solution)/shard_map/while/body/eval_jaxpr/ppermute | solution.py:11
  469.0 15.1 %conditional.2 = (bf16[128,3584]{1,0:T(8,128)(2,1)}) conditional(s32[]{:T(128)} %convert_element_type.57, () %tuple.55, (bf16[128,3584]{1,0:T(8,128)(2,1)S(1)}, bf16[3584,3584]{1,0:T(8,128)(2,1)}, bf16[16,3584]{1,0:T(8,128)(2,1)S(1)}, bf16[16,3584]{1,0:T(8,128)(2,1)S(1)}) %tuple.56), branch_computations={%region_2.2_spmd, %region_3.3_spmd} | conditional | flops 3318614016 | bytes 32342024 | solution.py:103
  469.0 12.9 %fusion.13 = f32[128,3584]{1,0:T(8,128)S(1)} fusion(bf16[128,3584]{1,0:T(8,128)(2,1)S(1)} %get-tuple-element.202, bf16[3584,3584]{1,0:T(8,128)(2,1)} %get-tuple-element.203), kind=kOutput, calls=%fused_computation.28 | convolution fusion | flops 3288334336 | bytes 28442624 | tf_op jit(solution)/shard_map/while/body/eval_jaxpr/cond/branch_1_fun/dot_general | solution.py:73
  485.4 3.3 collective-permute-done
  488.7 4.9 multiply_reduce_fusion.3
  493.6 4.9 multiply_reduce_fusion.2
  498.5 13.5 %all_to_all.11 = f32[8,1,4]{2,1,0:T(1,128)S(1)} all-to-all(f32[8,1,4]{2,1,0:T(1,128)S(1)} %broadcast_in_dim.36), channel_id=1, replica_groups=mesh['section'=8,'dp'=16] {'section'}, dimensions={0} | all-to-all | bytes 256 | tf_op jit(solution)/shard_map/all_to_all | solution.py:16
  513.7 5.3 all-to-all-start.1
  519.6 10.9 %all-to-all-done.1 = f32[16,32,224]{2,1,0:T(8,128)S(1)} async-done(((f32[16,32,224]{2,1,0:T(8,128)}), f32[16,32,224]{2,1,0:T(8,128)S(1)}, u32[]{:S(2)}, u32[]{:S(2)}) %all-to-all-start.1) | async-done | bytes 458784 | tf_op jit(solution)/shard_map/all_to_all | solution.py:33
  (69 shorter events, 73.1 us)
Async XLA Ops:
  7.2 162.4 %all-gather.3.cloned.1.call-start = ((), (), s32[]{:S(2)}) async-start(), calls=%async_computation.2 | async-start | bytes 27295744 | tf_op jit(solution)/shard_map/all_gather | solution.py:67
  13.0 158.7 %copy-start = (bf16[1,16,3584]{2,1,0:T(8,128)(2,1)S(1)}, bf16[1,16,3584]{2,1,0:T(8,128)(2,1)}, u32[]{:S(2)}) copy-start(bf16[1,16,3584]{2,1,0:T(8,128)(2,1)} %param.15) | copy-start | bytes 344068
  13.0 158.7 %copy-start.1 = (bf16[1,16,3584]{2,1,0:T(8,128)(2,1)S(1)}, bf16[1,16,3584]{2,1,0:T(8,128)(2,1)}, u32[]{:S(2)}) copy-start(bf16[1,16,3584]{2,1,0:T(8,128)(2,1)} %param.14) | copy-start | bytes 344068
  176.6 4.6 collective-permute-start
  186.1 14.3 %collective-permute-start = (bf16[128,3584]{1,0:T(8,128)(2,1)}, bf16[128,3584]{1,0:T(8,128)(2,1)S(1)}, u32[]{:S(2)}, u32[]{:S(2)}) collective-permute-start(bf16[128,3584]{1,0:T(8,128)(2,1)} %get-tuple-element.349), channel_id=1, source_target_pairs={{16,0},{32,16},{48,32},{64,48},{80,64},{96,80},{112,96},{17,1},{33... | collective-permute-start | bytes 2752520 | tf_op jit(solution)/shard_map/while/body/eval_jaxpr/ppermute | solution.py:11
  205.2 14.9 %collective-permute-start = (bf16[128,3584]{1,0:T(8,128)(2,1)}, bf16[128,3584]{1,0:T(8,128)(2,1)S(1)}, u32[]{:S(2)}, u32[]{:S(2)}) collective-permute-start(bf16[128,3584]{1,0:T(8,128)(2,1)} %get-tuple-element.349), channel_id=1, source_target_pairs={{16,0},{32,16},{48,32},{64,48},{80,64},{96,80},{112,96},{17,1},{33... | collective-permute-start | bytes 2752520 | tf_op jit(solution)/shard_map/while/body/eval_jaxpr/ppermute | solution.py:11
  225.0 14.9 %collective-permute-start = (bf16[128,3584]{1,0:T(8,128)(2,1)}, bf16[128,3584]{1,0:T(8,128)(2,1)S(1)}, u32[]{:S(2)}, u32[]{:S(2)}) collective-permute-start(bf16[128,3584]{1,0:T(8,128)(2,1)} %get-tuple-element.349), channel_id=1, source_target_pairs={{16,0},{32,16},{48,32},{64,48},{80,64},{96,80},{112,96},{17,1},{33... | collective-permute-start | bytes 2752520 | tf_op jit(solution)/shard_map/while/body/eval_jaxpr/ppermute | solution.py:11
  244.8 14.9 %collective-permute-start = (bf16[128,3584]{1,0:T(8,128)(2,1)}, bf16[128,3584]{1,0:T(8,128)(2,1)S(1)}, u32[]{:S(2)}, u32[]{:S(2)}) collective-permute-start(bf16[128,3584]{1,0:T(8,128)(2,1)} %get-tuple-element.349), channel_id=1, source_target_pairs={{16,0},{32,16},{48,32},{64,48},{80,64},{96,80},{112,96},{17,1},{33... | collective-permute-start | bytes 2752520 | tf_op jit(solution)/shard_map/while/body/eval_jaxpr/ppermute | solution.py:11
  264.6 14.9 %collective-permute-start = (bf16[128,3584]{1,0:T(8,128)(2,1)}, bf16[128,3584]{1,0:T(8,128)(2,1)S(1)}, u32[]{:S(2)}, u32[]{:S(2)}) collective-permute-start(bf16[128,3584]{1,0:T(8,128)(2,1)} %get-tuple-element.349), channel_id=1, source_target_pairs={{16,0},{32,16},{48,32},{64,48},{80,64},{96,80},{112,96},{17,1},{33... | collective-permute-start | bytes 2752520 | tf_op jit(solution)/shard_map/while/body/eval_jaxpr/ppermute | solution.py:11
  284.4 79.4 %collective-permute-start = (bf16[128,3584]{1,0:T(8,128)(2,1)}, bf16[128,3584]{1,0:T(8,128)(2,1)S(1)}, u32[]{:S(2)}, u32[]{:S(2)}) collective-permute-start(bf16[128,3584]{1,0:T(8,128)(2,1)} %get-tuple-element.349), channel_id=1, source_target_pairs={{16,0},{32,16},{48,32},{64,48},{80,64},{96,80},{112,96},{17,1},{33... | collective-permute-start | bytes 2752520 | tf_op jit(solution)/shard_map/while/body/eval_jaxpr/ppermute | solution.py:11
  382.7 14.9 %collective-permute-start = (bf16[128,3584]{1,0:T(8,128)(2,1)}, bf16[128,3584]{1,0:T(8,128)(2,1)S(1)}, u32[]{:S(2)}, u32[]{:S(2)}) collective-permute-start(bf16[128,3584]{1,0:T(8,128)(2,1)} %get-tuple-element.349), channel_id=1, source_target_pairs={{16,0},{32,16},{48,32},{64,48},{80,64},{96,80},{112,96},{17,1},{33... | collective-permute-start | bytes 2752520 | tf_op jit(solution)/shard_map/while/body/eval_jaxpr/ppermute | solution.py:11
  416.5 14.9 %collective-permute-start = (bf16[128,3584]{1,0:T(8,128)(2,1)}, bf16[128,3584]{1,0:T(8,128)(2,1)S(1)}, u32[]{:S(2)}, u32[]{:S(2)}) collective-permute-start(bf16[128,3584]{1,0:T(8,128)(2,1)} %get-tuple-element.349), channel_id=1, source_target_pairs={{16,0},{32,16},{48,32},{64,48},{80,64},{96,80},{112,96},{17,1},{33... | collective-permute-start | bytes 2752520 | tf_op jit(solution)/shard_map/while/body/eval_jaxpr/ppermute | solution.py:11
  450.3 14.9 %collective-permute-start = (bf16[128,3584]{1,0:T(8,128)(2,1)}, bf16[128,3584]{1,0:T(8,128)(2,1)S(1)}, u32[]{:S(2)}, u32[]{:S(2)}) collective-permute-start(bf16[128,3584]{1,0:T(8,128)(2,1)} %get-tuple-element.349), channel_id=1, source_target_pairs={{16,0},{32,16},{48,32},{64,48},{80,64},{96,80},{112,96},{17,1},{33... | collective-permute-start | bytes 2752520 | tf_op jit(solution)/shard_map/while/body/eval_jaxpr/ppermute | solution.py:11
  484.1 4.6 collective-permute-start
  498.4 20.5 %copy-start.2 = (s32[1,4]{1,0:T(1,128)S(1)}, s32[1,4]{1,0:T(1,128)}, u32[]{:S(2)}) copy-start(s32[1,4]{1,0:T(1,128)} %param.16) | copy-start | bytes 52
  513.7 16.8 %all-to-all-start.1 = ((f32[16,32,224]{2,1,0:T(8,128)}), f32[16,32,224]{2,1,0:T(8,128)S(1)}, u32[]{:S(2)}, u32[]{:S(2)}) async-start(f32[16,32,224]{2,1,0:T(8,128)} %copy.13), calls=%async_computation.1 | async-start | bytes 1048576 | tf_op jit(solution)/shard_map/all_to_all | solution.py:33
Sparse Core Ops, SparseCore 0:
  10.1 159.3 all-gather.2
where the time goes:
time: 539 us; the launch traced here: 538 us
  waiting for transfers between devices  361 us (67%)
  matrix products  70.1 us (13%)
  other arithmetic  34.6 us (6%)
  local copies, waits for them, and re-layouts  25 us (5%)
  starting transfers between devices  19.4 us (4%)
  between operations  14.1 us (3%)
  blocking collectives  13.5 us (3%)
    ppermute x11, waiting for transfers between devices, from_behind(): lax.ppermute(value, axis, [(source, source + steps) for source in range(f...  193 us
    all_gather x1, waiting for transfers between devices, on_device(): weight = lax.all_gather(frozen[0], 'dp', axis=0, tiled=True)  157 us
    dot_general x4, matrix products, backstep(): in_grad = jnp.dot(out_grad, weight.T, preferred_element_type=jnp.float32)  51.6 us
    dynamic_update_slice x11, other arithmetic, tick_step(): lax.dynamic_update_index_in_dim(stored_grads, kept, held_index, 0)  28.6 us
    ppermute x11, starting transfers between devices, from_behind(): lax.ppermute(value, axis, [(source, source + steps) for source in range(f...  14.1 us
    dynamic_slice x11, local copies, waits for them, and re-layouts, tick_step(): lax.dynamic_index_in_dim(stored_grads, held_index, 0, keepdims=False)  13.6 us
    all_to_all x1, blocking collectives, sent_to_all(): lax.all_to_all(jnp.broadcast_to(value[None], (size, *value.shape)), axis,...  13.5 us
    all_to_all x1, waiting for transfers between devices, sent_and_summed(): lax.all_to_all(pieces, axis, split_axis=0, concat_axis=0, tiled=True)  10.9 us
  transfers between devices with their start and end apart: 13, of which 13 were waited for; matrix products, arithmetic and copies ran while one was open for 1% of the time, Pallas kernels for 0%

commit v1 on v0

--- a/solution.py
+++ b/solution.py
@@ -64,7 +64,12 @@
     seeded = cotangent.reshape(slot_count, positions, features) * live_mask[:, :, None]
     input_blocks = layer_inputs.reshape(slot_count, positions, features)
     clip_scale = math.sqrt(2.0 * rank_size * features) / math.sqrt(replica_count * slot_count)
-    weight = lax.all_gather(frozen[0], "dp", axis=0, tiled=True)
+    ring = [frozen[0]]
+    for hop in range(15):
+        ring.append(lax.ppermute(ring[-1], "dp", [(dev, (dev + 1) % 16) for dev in range(16)]))
+    weight = jnp.roll(
+        jnp.concatenate(ring[::-1], axis=0), (lax.axis_index("dp") + 1) * ring[0].shape[0], axis=0
+    )
 
     def backstep(out_grad):
         up_grad = jnp.dot(out_grad, up_rows.T, preferred_element_type=jnp.float32).astype(

time: 539 us -> 994 us (1.84)
  waiting for transfers between devices: 361 us -> 728 us
  local copies, waits for them, and re-layouts: 25 us -> 125 us
  between operations: 14.1 us -> 0.85 us
    ppermute x0 -> x15, waiting for transfers between devices: none -> 527 us  [on_device(): lax.ppermute(ring[-1], 'dp', [(dev, (dev + 1) % 16) for dev in range(16)])]
    all_gather x1 -> x0, waiting for transfers between devices: 157 us -> none  [on_device(): weight = lax.all_gather(frozen[0], 'dp', axis=0, tiled=True)]
    unnamed x6 -> x87, local copies, waits for them, and re-layouts: 0.01 us -> 76.6 us
    dynamic_slice x0 -> x1, local copies, waits for them, and re-layouts: none -> 22.7 us  [on_device(): jnp.roll(jnp.concatenate(ring[::-1], axis=0), (lax.axis_index('dp') + 1)...]
  transfers between devices with their start and end apart: 13 -> 27, of which waited for: 13 -> 27; matrix products, arithmetic and copies ran while one was open for 1% -> 1% of each run, Pallas kernels for 0% -> 0%
where the time goes in v1:
time: 994 us; the launch traced here: 992 us
  waiting for transfers between devices  728 us (73%)
  local copies, waits for them, and re-layouts  125 us (13%)
  matrix products  70 us (7%)
  other arithmetic  35.1 us (4%)
  starting transfers between devices  19.4 us (2%)
  blocking collectives  13.5 us (1%)
    ppermute x15, waiting for transfers between devices, on_device(): lax.ppermute(ring[-1], 'dp', [(dev, (dev + 1) % 16) for dev in range(16)])  527 us
    ppermute x11, waiting for transfers between devices, from_behind(): lax.ppermute(value, axis, [(source, source + steps) for source in range(f...  189 us
    unnamed x87, local copies, waits for them, and re-layouts  76.6 us
    dot_general x4, matrix products, backstep(): in_grad = jnp.dot(out_grad, weight.T, preferred_element_type=jnp.float32)  51.6 us
    dynamic_update_slice x11, other arithmetic, tick_step(): lax.dynamic_update_index_in_dim(stored_grads, kept, held_index, 0)  28.2 us
    dynamic_slice x1, local copies, waits for them, and re-layouts, on_device(): jnp.roll(jnp.concatenate(ring[::-1], axis=0), (lax.axis_index('dp') + 1)...  22.7 us
  transfers between devices with their start and end apart: 27, of which 27 were waited for; matrix products, arithmetic and copies ran while one was open for 1% of the time, Pallas kernels for 0%

profile of v1, /device:TPU:0, one launch (start us, length us, event | category | flops | bytes accessed | tf_op | source)
XLA Modules:
  0.0 992.1 jit_solution(3198674275811002785)
XLA Ops:
  2.3 40.0 %collective-permute-done.1 = bf16[224,3584]{1,0:T(8,128)(2,1)S(1)} collective-permute-done((bf16[224,3584]{1,0:T(8,128)(2,1)}, bf16[224,3584]{1,0:T(8,128)(2,1)S(1)}, u32[]{:S(2)}, u32[]{:S(2)}) %collective-permute-start.1) | collective-permute-done | bytes 1605664 | tf_op jit(solution)/shard_map/ppermute | solution.py:69
  42.4 39.6 %collective-permute-done.2 = bf16[224,3584]{1,0:T(8,128)(2,1)S(1)} collective-permute-done((bf16[224,3584]{1,0:T(8,128)(2,1)S(1)}, bf16[224,3584]{1,0:T(8,128)(2,1)S(1)}, u32[]{:S(2)}, u32[]{:S(2)}) %collective-permute-start.2) | collective-permute-done | bytes 1605664 | tf_op jit(solution)/shard_map/ppermute | solution.py:69
  83.1 38.7 %collective-permute-done.3 = bf16[224,3584]{1,0:T(8,128)(2,1)S(1)} collective-permute-done((bf16[224,3584]{1,0:T(8,128)(2,1)S(1)}, bf16[224,3584]{1,0:T(8,128)(2,1)S(1)}, u32[]{:S(2)}, u32[]{:S(2)}) %collective-permute-start.3) | collective-permute-done | bytes 1605664 | tf_op jit(solution)/shard_map/ppermute | solution.py:69
  123.0 37.9 %collective-permute-done.4 = bf16[224,3584]{1,0:T(8,128)(2,1)S(1)} collective-permute-done((bf16[224,3584]{1,0:T(8,128)(2,1)S(1)}, bf16[224,3584]{1,0:T(8,128)(2,1)S(1)}, u32[]{:S(2)}, u32[]{:S(2)}) %collective-permute-start.4) | collective-permute-done | bytes 1605664 | tf_op jit(solution)/shard_map/ppermute | solution.py:69
  162.0 37.0 %collective-permute-done.5 = bf16[224,3584]{1,0:T(8,128)(2,1)S(1)} collective-permute-done((bf16[224,3584]{1,0:T(8,128)(2,1)S(1)}, bf16[224,3584]{1,0:T(8,128)(2,1)S(1)}, u32[]{:S(2)}, u32[]{:S(2)}) %collective-permute-start.5) | collective-permute-done | bytes 1605664 | tf_op jit(solution)/shard_map/ppermute | solution.py:69
  200.2 36.2 %collective-permute-done.6 = bf16[224,3584]{1,0:T(8,128)(2,1)S(1)} collective-permute-done((bf16[224,3584]{1,0:T(8,128)(2,1)S(1)}, bf16[224,3584]{1,0:T(8,128)(2,1)S(1)}, u32[]{:S(2)}, u32[]{:S(2)}) %collective-permute-start.6) | collective-permute-done | bytes 1605664 | tf_op jit(solution)/shard_map/ppermute | solution.py:69
  237.5 35.3 %collective-permute-done.7 = bf16[224,3584]{1,0:T(8,128)(2,1)S(1)} collective-permute-done((bf16[224,3584]{1,0:T(8,128)(2,1)S(1)}, bf16[224,3584]{1,0:T(8,128)(2,1)S(1)}, u32[]{:S(2)}, u32[]{:S(2)}) %collective-permute-start.7) | collective-permute-done | bytes 1605664 | tf_op jit(solution)/shard_map/ppermute | solution.py:69
  274.0 34.4 %collective-permute-done.8 = bf16[224,3584]{1,0:T(8,128)(2,1)S(1)} collective-permute-done((bf16[224,3584]{1,0:T(8,128)(2,1)S(1)}, bf16[224,3584]{1,0:T(8,128)(2,1)S(1)}, u32[]{:S(2)}, u32[]{:S(2)}) %collective-permute-start.8) | collective-permute-done | bytes 1605664 | tf_op jit(solution)/shard_map/ppermute | solution.py:69
  309.7 34.1 %collective-permute-done.9 = bf16[224,3584]{1,0:T(8,128)(2,1)S(1)} collective-permute-done((bf16[224,3584]{1,0:T(8,128)(2,1)S(1)}, bf16[224,3584]{1,0:T(8,128)(2,1)S(1)}, u32[]{:S(2)}, u32[]{:S(2)}) %collective-permute-start.9) | collective-permute-done | bytes 1605664 | tf_op jit(solution)/shard_map/ppermute | solution.py:69
  344.9 34.1 %collective-permute-done.10 = bf16[224,3584]{1,0:T(8,128)(2,1)S(1)} collective-permute-done((bf16[224,3584]{1,0:T(8,128)(2,1)S(1)}, bf16[224,3584]{1,0:T(8,128)(2,1)S(1)}, u32[]{:S(2)}, u32[]{:S(2)}) %collective-permute-start.10) | collective-permute-done | bytes 1605664 | tf_op jit(solution)/shard_map/ppermute | solution.py:69
  380.2 34.1 %collective-permute-done.11 = bf16[224,3584]{1,0:T(8,128)(2,1)S(1)} collective-permute-done((bf16[224,3584]{1,0:T(8,128)(2,1)S(1)}, bf16[224,3584]{1,0:T(8,128)(2,1)S(1)}, u32[]{:S(2)}, u32[]{:S(2)}) %collective-permute-start.11) | collective-permute-done | bytes 1605664 | tf_op jit(solution)/shard_map/ppermute | solution.py:69
  415.5 34.1 %collective-permute-done.12 = bf16[224,3584]{1,0:T(8,128)(2,1)S(1)} collective-permute-done((bf16[224,3584]{1,0:T(8,128)(2,1)S(1)}, bf16[224,3584]{1,0:T(8,128)(2,1)S(1)}, u32[]{:S(2)}, u32[]{:S(2)}) %collective-permute-start.12) | collective-permute-done | bytes 1605664 | tf_op jit(solution)/shard_map/ppermute | solution.py:69
  450.7 34.1 %collective-permute-done.13 = bf16[224,3584]{1,0:T(8,128)(2,1)S(1)} collective-permute-done((bf16[224,3584]{1,0:T(8,128)(2,1)S(1)}, bf16[224,3584]{1,0:T(8,128)(2,1)S(1)}, u32[]{:S(2)}, u32[]{:S(2)}) %collective-permute-start.13) | collective-permute-done | bytes 1605664 | tf_op jit(solution)/shard_map/ppermute | solution.py:69
  486.0 35.0 %collective-permute-done.14 = bf16[224,3584]{1,0:T(8,128)(2,1)} collective-permute-done((bf16[224,3584]{1,0:T(8,128)(2,1)S(1)}, bf16[224,3584]{1,0:T(8,128)(2,1)}, u32[]{:S(2)}, u32[]{:S(2)}) %collective-permute-start.14) | collective-permute-done | bytes 1605664 | tf_op jit(solution)/shard_map/ppermute | solution.py:69
  527.1 22.7 %collective-permute-done.15 = bf16[224,3584]{1,0:T(8,128)(2,1)} collective-permute-done((bf16[224,3584]{1,0:T(8,128)(2,1)}, bf16[224,3584]{1,0:T(8,128)(2,1)}, u32[]{:S(2)}, u32[]{:S(2)}) %collective-permute-start.15) | collective-permute-done | bytes 1605664 | tf_op jit(solution)/shard_map/ppermute | solution.py:69
  613.6 22.7 %constant_dynamic-slice_fusion.1 = bf16[3584,3584]{1,0:T(8,128)(2,1)} fusion(bf16[7168,3584]{1,0:T(8,128)(2,1)} %constant_dynamic-update-slice_fusion, s32[]{:T(128)S(6)} %select_n.59), kind=kLoop, calls=%fused_computation.59 | loop fusion | bytes 51380228 | tf_op jit(solution)/shard_map/jit(_roll_dynamic)/dynamic_slice | solution.py:70
  638.5 312.6 %while.17 = (s32[]{:T(128)}, bf16[128,3584]{1,0:T(8,128)(2,1)S(1)}, bf16[4,128,3584]{2,1,0:T(8,128)(2,1)}, s32[]{:T(128)}, pred[]{:T(512)}, /*index=5*/bf16[4,12...) while((s32[]{:T(128)}, bf16[128,3584]{1,0:T(8,128)(2,1)S(1)}, ...), condition=%wide.region_4.5_spmd, body=%wide.region_1.4_spmd.sunk | while | flops 3319531520 | bytes 42435348 | solution.py:116
  654.0 13.1 %collective-permute-done = bf16[128,3584]{1,0:T(8,128)(2,1)S(1)} collective-permute-done((bf16[128,3584]{1,0:T(8,128)(2,1)}, bf16[128,3584]{1,0:T(8,128)(2,1)S(1)}, u32[]{:S(2)}, u32[]{:S(2)}) %collective-permute-start) | collective-permute-done | bytes 917536 | tf_op jit(solution)/shard_map/while/body/eval_jaxpr/ppermute | solution.py:11
  673.1 13.6 %collective-permute-done = bf16[128,3584]{1,0:T(8,128)(2,1)S(1)} collective-permute-done((bf16[128,3584]{1,0:T(8,128)(2,1)}, bf16[128,3584]{1,0:T(8,128)(2,1)S(1)}, u32[]{:S(2)}, u32[]{:S(2)}) %collective-permute-start) | collective-permute-done | bytes 917536 | tf_op jit(solution)/shard_map/while/body/eval_jaxpr/ppermute | solution.py:11
  692.9 13.6 %collective-permute-done = bf16[128,3584]{1,0:T(8,128)(2,1)S(1)} collective-permute-done((bf16[128,3584]{1,0:T(8,128)(2,1)}, bf16[128,3584]{1,0:T(8,128)(2,1)S(1)}, u32[]{:S(2)}, u32[]{:S(2)}) %collective-permute-start) | collective-permute-done | bytes 917536 | tf_op jit(solution)/shard_map/while/body/eval_jaxpr/ppermute | solution.py:11
  712.6 13.6 %collective-permute-done = bf16[128,3584]{1,0:T(8,128)(2,1)S(1)} collective-permute-done((bf16[128,3584]{1,0:T(8,128)(2,1)}, bf16[128,3584]{1,0:T(8,128)(2,1)S(1)}, u32[]{:S(2)}, u32[]{:S(2)}) %collective-permute-start) | collective-permute-done | bytes 917536 | tf_op jit(solution)/shard_map/while/body/eval_jaxpr/ppermute | solution.py:11
  732.3 13.6 %collective-permute-done = bf16[128,3584]{1,0:T(8,128)(2,1)S(1)} collective-permute-done((bf16[128,3584]{1,0:T(8,128)(2,1)}, bf16[128,3584]{1,0:T(8,128)(2,1)S(1)}, u32[]{:S(2)}, u32[]{:S(2)}) %collective-permute-start) | collective-permute-done | bytes 917536 | tf_op jit(solution)/shard_map/while/body/eval_jaxpr/ppermute | solution.py:11
  752.0 74.2 %collective-permute-done = bf16[128,3584]{1,0:T(8,128)(2,1)S(1)} collective-permute-done((bf16[128,3584]{1,0:T(8,128)(2,1)}, bf16[128,3584]{1,0:T(8,128)(2,1)S(1)}, u32[]{:S(2)}, u32[]{:S(2)}) %collective-permute-start) | collective-permute-done | bytes 917536 | tf_op jit(solution)/shard_map/while/body/eval_jaxpr/ppermute | solution.py:11
  830.0 15.1 %conditional.2 = (bf16[128,3584]{1,0:T(8,128)(2,1)}) conditional(s32[]{:T(128)} %convert_element_type.57, () %tuple.55, (bf16[128,3584]{1,0:T(8,128)(2,1)S(1)}, bf16[3584,3584]{1,0:T(8,128)(2,1)}, bf16[16,3584]{1,0:T(8,128)(2,1)S(1)}, bf16[16,3584]{1,0:T(8,128)(2,1)S(1)}) %tuple.56), branch_computations={%region_2.2_spmd, %region_3.3_spmd} | conditional | flops 3318614016 | bytes 32342024 | solution.py:108
  846.4 13.6 %collective-permute-done = bf16[128,3584]{1,0:T(8,128)(2,1)S(1)} collective-permute-done((bf16[128,3584]{1,0:T(8,128)(2,1)}, bf16[128,3584]{1,0:T(8,128)(2,1)S(1)}, u32[]{:S(2)}, u32[]{:S(2)}) %collective-permute-start) | collective-permute-done | bytes 917536 | tf_op jit(solution)/shard_map/while/body/eval_jaxpr/ppermute | solution.py:11
  863.8 15.1 %conditional.2 = (bf16[128,3584]{1,0:T(8,128)(2,1)}) conditional(s32[]{:T(128)} %convert_element_type.57, () %tuple.55, (bf16[128,3584]{1,0:T(8,128)(2,1)S(1)}, bf16[3584,3584]{1,0:T(8,128)(2,1)}, bf16[16,3584]{1,0:T(8,128)(2,1)S(1)}, bf16[16,3584]{1,0:T(8,128)(2,1)S(1)}) %tuple.56), branch_computations={%region_2.2_spmd, %region_3.3_spmd} | conditional | flops 3318614016 | bytes 32342024 | solution.py:108
  880.1 13.6 %collective-permute-done = bf16[128,3584]{1,0:T(8,128)(2,1)S(1)} collective-permute-done((bf16[128,3584]{1,0:T(8,128)(2,1)}, bf16[128,3584]{1,0:T(8,128)(2,1)S(1)}, u32[]{:S(2)}, u32[]{:S(2)}) %collective-permute-start) | collective-permute-done | bytes 917536 | tf_op jit(solution)/shard_map/while/body/eval_jaxpr/ppermute | solution.py:11
  897.6 15.1 %conditional.2 = (bf16[128,3584]{1,0:T(8,128)(2,1)}) conditional(s32[]{:T(128)} %convert_element_type.57, () %tuple.55, (bf16[128,3584]{1,0:T(8,128)(2,1)S(1)}, bf16[3584,3584]{1,0:T(8,128)(2,1)}, bf16[16,3584]{1,0:T(8,128)(2,1)S(1)}, bf16[16,3584]{1,0:T(8,128)(2,1)S(1)}) %tuple.56), branch_computations={%region_2.2_spmd, %region_3.3_spmd} | conditional | flops 3318614016 | bytes 32342024 | solution.py:108
  913.9 13.6 %collective-permute-done = bf16[128,3584]{1,0:T(8,128)(2,1)S(1)} collective-permute-done((bf16[128,3584]{1,0:T(8,128)(2,1)}, bf16[128,3584]{1,0:T(8,128)(2,1)S(1)}, u32[]{:S(2)}, u32[]{:S(2)}) %collective-permute-start) | collective-permute-done | bytes 917536 | tf_op jit(solution)/shard_map/while/body/eval_jaxpr/ppermute | solution.py:11
  931.4 15.1 %conditional.2 = (bf16[128,3584]{1,0:T(8,128)(2,1)}) conditional(s32[]{:T(128)} %convert_element_type.57, () %tuple.55, (bf16[128,3584]{1,0:T(8,128)(2,1)S(1)}, bf16[3584,3584]{1,0:T(8,128)(2,1)}, bf16[16,3584]{1,0:T(8,128)(2,1)S(1)}, bf16[16,3584]{1,0:T(8,128)(2,1)S(1)}) %tuple.56), branch_computations={%region_2.2_spmd, %region_3.3_spmd} | conditional | flops 3318614016 | bytes 32342024 | solution.py:108
  931.4 12.9 %fusion.13 = f32[128,3584]{1,0:T(8,128)S(1)} fusion(bf16[128,3584]{1,0:T(8,128)(2,1)S(1)} %get-tuple-element.202, bf16[3584,3584]{1,0:T(8,128)(2,1)} %get-tuple-element.203), kind=kOutput, calls=%fused_computation.61 | convolution fusion | flops 3288334336 | bytes 28442624 | tf_op jit(solution)/shard_map/while/body/eval_jaxpr/cond/branch_1_fun/dot_general | solution.py:78
  960.8 13.5 %all_to_all.11 = f32[8,1,4]{2,1,0:T(1,128)S(1)} all-to-all(f32[8,1,4]{2,1,0:T(1,128)S(1)} %broadcast_in_dim.36), channel_id=1, replica_groups=mesh['section'=8,'dp'=16] {'section'}, dimensions={0} | all-to-all | bytes 256 | tf_op jit(solution)/shard_map/all_to_all | solution.py:16
  (179 shorter events, 238.9 us)
Async XLA Ops:
  0.6 588.3 %copy-start = (bf16[1,224,3584]{2,1,0:T(8,128)(2,1)S(1)}, bf16[1,224,3584]{2,1,0:T(8,128)(2,1)}, u32[]{:S(2)}) copy-start(bf16[1,224,3584]{2,1,0:T(8,128)(2,1)} %param.13) | copy-start | bytes 4816900
  0.6 41.7 %collective-permute-start.1 = (bf16[224,3584]{1,0:T(8,128)(2,1)}, bf16[224,3584]{1,0:T(8,128)(2,1)S(1)}, u32[]{:S(2)}, u32[]{:S(2)}) collective-permute-start(bf16[224,3584]{1,0:T(8,128)(2,1)} %bitcast.51), channel_id=1, source_target_pairs={{0,1},{1,2},{2,3},{3,4},{4,5},{5,6},{6,7},{7,8},{8,9},{9,10},{10,1... | collective-permute-start | bytes 4816904 | tf_op jit(solution)/shard_map/ppermute | solution.py:69
  42.4 39.6 %collective-permute-start.2 = (bf16[224,3584]{1,0:T(8,128)(2,1)S(1)}, bf16[224,3584]{1,0:T(8,128)(2,1)S(1)}, u32[]{:S(2)}, u32[]{:S(2)}) collective-permute-start(bf16[224,3584]{1,0:T(8,128)(2,1)S(1)} %collective-permute-done.1), channel_id=1, source_target_pairs={{0,1},{1,2},{2,3},{3,4},{4,5},{5,6},{6,7},{7,8},{8,9},{9,10},{10,1... | collective-permute-start | bytes 4816904 | tf_op jit(solution)/shard_map/ppermute | solution.py:69
  83.1 38.7 %collective-permute-start.3 = (bf16[224,3584]{1,0:T(8,128)(2,1)S(1)}, bf16[224,3584]{1,0:T(8,128)(2,1)S(1)}, u32[]{:S(2)}, u32[]{:S(2)}) collective-permute-start(bf16[224,3584]{1,0:T(8,128)(2,1)S(1)} %collective-permute-done.2), channel_id=1, source_target_pairs={{0,1},{1,2},{2,3},{3,4},{4,5},{5,6},{6,7},{7,8},{8,9},{9,10},{10,1... | collective-permute-start | bytes 4816904 | tf_op jit(solution)/shard_map/ppermute | solution.py:69
  123.0 37.9 %collective-permute-start.4 = (bf16[224,3584]{1,0:T(8,128)(2,1)S(1)}, bf16[224,3584]{1,0:T(8,128)(2,1)S(1)}, u32[]{:S(2)}, u32[]{:S(2)}) collective-permute-start(bf16[224,3584]{1,0:T(8,128)(2,1)S(1)} %collective-permute-done.3), channel_id=1, source_target_pairs={{0,1},{1,2},{2,3},{3,4},{4,5},{5,6},{6,7},{7,8},{8,9},{9,10},{10,1... | collective-permute-start | bytes 4816904 | tf_op jit(solution)/shard_map/ppermute | solution.py:69
  162.0 37.0 %collective-permute-start.5 = (bf16[224,3584]{1,0:T(8,128)(2,1)S(1)}, bf16[224,3584]{1,0:T(8,128)(2,1)S(1)}, u32[]{:S(2)}, u32[]{:S(2)}) collective-permute-start(bf16[224,3584]{1,0:T(8,128)(2,1)S(1)} %collective-permute-done.4), channel_id=1, source_target_pairs={{0,1},{1,2},{2,3},{3,4},{4,5},{5,6},{6,7},{7,8},{8,9},{9,10},{10,1... | collective-permute-start | bytes 4816904 | tf_op jit(solution)/shard_map/ppermute | solution.py:69
  200.2 36.2 %collective-permute-start.6 = (bf16[224,3584]{1,0:T(8,128)(2,1)S(1)}, bf16[224,3584]{1,0:T(8,128)(2,1)S(1)}, u32[]{:S(2)}, u32[]{:S(2)}) collective-permute-start(bf16[224,3584]{1,0:T(8,128)(2,1)S(1)} %collective-permute-done.5), channel_id=1, source_target_pairs={{0,1},{1,2},{2,3},{3,4},{4,5},{5,6},{6,7},{7,8},{8,9},{9,10},{10,1... | collective-permute-start | bytes 4816904 | tf_op jit(solution)/shard_map/ppermute | solution.py:69
  237.5 35.3 %collective-permute-start.7 = (bf16[224,3584]{1,0:T(8,128)(2,1)S(1)}, bf16[224,3584]{1,0:T(8,128)(2,1)S(1)}, u32[]{:S(2)}, u32[]{:S(2)}) collective-permute-start(bf16[224,3584]{1,0:T(8,128)(2,1)S(1)} %collective-permute-done.6), channel_id=1, source_target_pairs={{0,1},{1,2},{2,3},{3,4},{4,5},{5,6},{6,7},{7,8},{8,9},{9,10},{10,1... | collective-permute-start | bytes 4816904 | tf_op jit(solution)/shard_map/ppermute | solution.py:69
  274.0 34.4 %collective-permute-start.8 = (bf16[224,3584]{1,0:T(8,128)(2,1)S(1)}, bf16[224,3584]{1,0:T(8,128)(2,1)S(1)}, u32[]{:S(2)}, u32[]{:S(2)}) collective-permute-start(bf16[224,3584]{1,0:T(8,128)(2,1)S(1)} %collective-permute-done.7), channel_id=1, source_target_pairs={{0,1},{1,2},{2,3},{3,4},{4,5},{5,6},{6,7},{7,8},{8,9},{9,10},{10,1... | collective-permute-start | bytes 4816904 | tf_op jit(solution)/shard_map/ppermute | solution.py:69
  309.7 34.1 %collective-permute-start.9 = (bf16[224,3584]{1,0:T(8,128)(2,1)S(1)}, bf16[224,3584]{1,0:T(8,128)(2,1)S(1)}, u32[]{:S(2)}, u32[]{:S(2)}) collective-permute-start(bf16[224,3584]{1,0:T(8,128)(2,1)S(1)} %collective-permute-done.8), channel_id=1, source_target_pairs={{0,1},{1,2},{2,3},{3,4},{4,5},{5,6},{6,7},{7,8},{8,9},{9,10},{10,1... | collective-permute-start | bytes 4816904 | tf_op jit(solution)/shard_map/ppermute | solution.py:69
  344.9 34.1 %collective-permute-start.10 = (bf16[224,3584]{1,0:T(8,128)(2,1)S(1)}, bf16[224,3584]{1,0:T(8,128)(2,1)S(1)}, u32[]{:S(2)}, u32[]{:S(2)}) collective-permute-start(bf16[224,3584]{1,0:T(8,128)(2,1)S(1)} %collective-permute-done.9), channel_id=1, source_target_pairs={{0,1},{1,2},{2,3},{3,4},{4,5},{5,6},{6,7},{7,8},{8,9},{9,10},{10,1... | collective-permute-start | bytes 4816904 | tf_op jit(solution)/shard_map/ppermute | solution.py:69
  380.2 34.1 %collective-permute-start.11 = (bf16[224,3584]{1,0:T(8,128)(2,1)S(1)}, bf16[224,3584]{1,0:T(8,128)(2,1)S(1)}, u32[]{:S(2)}, u32[]{:S(2)}) collective-permute-start(bf16[224,3584]{1,0:T(8,128)(2,1)S(1)} %collective-permute-done.10), channel_id=1, source_target_pairs={{0,1},{1,2},{2,3},{3,4},{4,5},{5,6},{6,7},{7,8},{8,9},{9,10},{10,1... | collective-permute-start | bytes 4816904 | tf_op jit(solution)/shard_map/ppermute | solution.py:69
  415.5 34.1 %collective-permute-start.12 = (bf16[224,3584]{1,0:T(8,128)(2,1)S(1)}, bf16[224,3584]{1,0:T(8,128)(2,1)S(1)}, u32[]{:S(2)}, u32[]{:S(2)}) collective-permute-start(bf16[224,3584]{1,0:T(8,128)(2,1)S(1)} %collective-permute-done.11), channel_id=1, source_target_pairs={{0,1},{1,2},{2,3},{3,4},{4,5},{5,6},{6,7},{7,8},{8,9},{9,10},{10,1... | collective-permute-start | bytes 4816904 | tf_op jit(solution)/shard_map/ppermute | solution.py:69
  450.7 34.1 %collective-permute-start.13 = (bf16[224,3584]{1,0:T(8,128)(2,1)S(1)}, bf16[224,3584]{1,0:T(8,128)(2,1)S(1)}, u32[]{:S(2)}, u32[]{:S(2)}) collective-permute-start(bf16[224,3584]{1,0:T(8,128)(2,1)S(1)} %collective-permute-done.12), channel_id=1, source_target_pairs={{0,1},{1,2},{2,3},{3,4},{4,5},{5,6},{6,7},{7,8},{8,9},{9,10},{10,1... | collective-permute-start | bytes 4816904 | tf_op jit(solution)/shard_map/ppermute | solution.py:69
  486.0 35.0 %collective-permute-start.14 = (bf16[224,3584]{1,0:T(8,128)(2,1)S(1)}, bf16[224,3584]{1,0:T(8,128)(2,1)}, u32[]{:S(2)}, u32[]{:S(2)}) collective-permute-start(bf16[224,3584]{1,0:T(8,128)(2,1)S(1)} %collective-permute-done.13), channel_id=1, source_target_pairs={{0,1},{1,2},{2,3},{3,4},{4,5},{5,6},{6,7},{7,8},{8,9},{9,10},{10,1... | collective-permute-start | bytes 4816904 | tf_op jit(solution)/shard_map/ppermute | solution.py:69
  521.0 28.8 %collective-permute-start.15 = (bf16[224,3584]{1,0:T(8,128)(2,1)}, bf16[224,3584]{1,0:T(8,128)(2,1)}, u32[]{:S(2)}, u32[]{:S(2)}) collective-permute-start(bf16[224,3584]{1,0:T(8,128)(2,1)} %collective-permute-done.14), channel_id=1, source_target_pairs={{0,1},{1,2},{2,3},{3,4},{4,5},{5,6},{6,7},{7,8},{8,9},{9,10},{10,1... | collective-permute-start | bytes 4816904 | tf_op jit(solution)/shard_map/ppermute | solution.py:69
  521.1 86.2 %copy-start.6 = (bf16[224,3584]{1,0:T(8,128)(2,1)S(1)}, bf16[224,3584]{1,0:T(8,128)(2,1)}, u32[]{:S(2)}) copy-start(bf16[224,3584]{1,0:T(8,128)(2,1)} %copy-done.5) | copy-start | bytes 4816900
  521.1 87.4 %copy-start.4 = (bf16[224,3584]{1,0:T(8,128)(2,1)S(1)}, bf16[224,3584]{1,0:T(8,128)(2,1)}, u32[]{:S(2)}) copy-start(bf16[224,3584]{1,0:T(8,128)(2,1)} %copy-done.3) | copy-start | bytes 4816900
  521.1 88.7 %copy-start.2 = (bf16[224,3584]{1,0:T(8,128)(2,1)S(1)}, bf16[224,3584]{1,0:T(8,128)(2,1)}, u32[]{:S(2)}) copy-start(bf16[224,3584]{1,0:T(8,128)(2,1)} %copy-done.1) | copy-start | bytes 4816900
  638.5 341.2 %copy-start.27 = (s32[1,4]{1,0:T(1,128)S(1)}, s32[1,4]{1,0:T(1,128)}, u32[]{:S(2)}) copy-start(s32[1,4]{1,0:T(1,128)} %param.16) | copy-start | bytes 52
  643.3 4.6 collective-permute-start
  652.7 14.4 %collective-permute-start = (bf16[128,3584]{1,0:T(8,128)(2,1)}, bf16[128,3584]{1,0:T(8,128)(2,1)S(1)}, u32[]{:S(2)}, u32[]{:S(2)}) collective-permute-start(bf16[128,3584]{1,0:T(8,128)(2,1)} %get-tuple-element.349), channel_id=1, source_target_pairs={{16,0},{32,16},{48,32},{64,48},{80,64},{96,80},{112,96},{17,1},{33... | collective-permute-start | bytes 2752520 | tf_op jit(solution)/shard_map/while/body/eval_jaxpr/ppermute | solution.py:11
  671.8 14.9 %collective-permute-start = (bf16[128,3584]{1,0:T(8,128)(2,1)}, bf16[128,3584]{1,0:T(8,128)(2,1)S(1)}, u32[]{:S(2)}, u32[]{:S(2)}) collective-permute-start(bf16[128,3584]{1,0:T(8,128)(2,1)} %get-tuple-element.349), channel_id=1, source_target_pairs={{16,0},{32,16},{48,32},{64,48},{80,64},{96,80},{112,96},{17,1},{33... | collective-permute-start | bytes 2752520 | tf_op jit(solution)/shard_map/while/body/eval_jaxpr/ppermute | solution.py:11
  691.6 14.9 %collective-permute-start = (bf16[128,3584]{1,0:T(8,128)(2,1)}, bf16[128,3584]{1,0:T(8,128)(2,1)S(1)}, u32[]{:S(2)}, u32[]{:S(2)}) collective-permute-start(bf16[128,3584]{1,0:T(8,128)(2,1)} %get-tuple-element.349), channel_id=1, source_target_pairs={{16,0},{32,16},{48,32},{64,48},{80,64},{96,80},{112,96},{17,1},{33... | collective-permute-start | bytes 2752520 | tf_op jit(solution)/shard_map/while/body/eval_jaxpr/ppermute | solution.py:11
  711.3 14.9 %collective-permute-start = (bf16[128,3584]{1,0:T(8,128)(2,1)}, bf16[128,3584]{1,0:T(8,128)(2,1)S(1)}, u32[]{:S(2)}, u32[]{:S(2)}) collective-permute-start(bf16[128,3584]{1,0:T(8,128)(2,1)} %get-tuple-element.349), channel_id=1, source_target_pairs={{16,0},{32,16},{48,32},{64,48},{80,64},{96,80},{112,96},{17,1},{33... | collective-permute-start | bytes 2752520 | tf_op jit(solution)/shard_map/while/body/eval_jaxpr/ppermute | solution.py:11
  731.0 14.9 %collective-permute-start = (bf16[128,3584]{1,0:T(8,128)(2,1)}, bf16[128,3584]{1,0:T(8,128)(2,1)S(1)}, u32[]{:S(2)}, u32[]{:S(2)}) collective-permute-start(bf16[128,3584]{1,0:T(8,128)(2,1)} %get-tuple-element.349), channel_id=1, source_target_pairs={{16,0},{32,16},{48,32},{64,48},{80,64},{96,80},{112,96},{17,1},{33... | collective-permute-start | bytes 2752520 | tf_op jit(solution)/shard_map/while/body/eval_jaxpr/ppermute | solution.py:11
  750.7 75.5 %collective-permute-start = (bf16[128,3584]{1,0:T(8,128)(2,1)}, bf16[128,3584]{1,0:T(8,128)(2,1)S(1)}, u32[]{:S(2)}, u32[]{:S(2)}) collective-permute-start(bf16[128,3584]{1,0:T(8,128)(2,1)} %get-tuple-element.349), channel_id=1, source_target_pairs={{16,0},{32,16},{48,32},{64,48},{80,64},{96,80},{112,96},{17,1},{33... | collective-permute-start | bytes 2752520 | tf_op jit(solution)/shard_map/while/body/eval_jaxpr/ppermute | solution.py:11
  845.1 14.9 %collective-permute-start = (bf16[128,3584]{1,0:T(8,128)(2,1)}, bf16[128,3584]{1,0:T(8,128)(2,1)S(1)}, u32[]{:S(2)}, u32[]{:S(2)}) collective-permute-start(bf16[128,3584]{1,0:T(8,128)(2,1)} %get-tuple-element.349), channel_id=1, source_target_pairs={{16,0},{32,16},{48,32},{64,48},{80,64},{96,80},{112,96},{17,1},{33... | collective-permute-start | bytes 2752520 | tf_op jit(solution)/shard_map/while/body/eval_jaxpr/ppermute | solution.py:11
  878.8 14.9 %collective-permute-start = (bf16[128,3584]{1,0:T(8,128)(2,1)}, bf16[128,3584]{1,0:T(8,128)(2,1)S(1)}, u32[]{:S(2)}, u32[]{:S(2)}) collective-permute-start(bf16[128,3584]{1,0:T(8,128)(2,1)} %get-tuple-element.349), channel_id=1, source_target_pairs={{16,0},{32,16},{48,32},{64,48},{80,64},{96,80},{112,96},{17,1},{33... | collective-permute-start | bytes 2752520 | tf_op jit(solution)/shard_map/while/body/eval_jaxpr/ppermute | solution.py:11
  912.6 14.9 %collective-permute-start = (bf16[128,3584]{1,0:T(8,128)(2,1)}, bf16[128,3584]{1,0:T(8,128)(2,1)S(1)}, u32[]{:S(2)}, u32[]{:S(2)}) collective-permute-start(bf16[128,3584]{1,0:T(8,128)(2,1)} %get-tuple-element.349), channel_id=1, source_target_pairs={{16,0},{32,16},{48,32},{64,48},{80,64},{96,80},{112,96},{17,1},{33... | collective-permute-start | bytes 2752520 | tf_op jit(solution)/shard_map/while/body/eval_jaxpr/ppermute | solution.py:11
  946.5 4.6 collective-permute-start
  976.1 15.3 %all-to-all-start.1 = ((f32[16,32,224]{2,1,0:T(8,128)}), f32[16,32,224]{2,1,0:T(8,128)S(1)}, u32[]{:S(2)}, u32[]{:S(2)}) async-start(f32[16,32,224]{2,1,0:T(8,128)} %copy.13), calls=%async_computation.1 | async-start | bytes 1048576 | tf_op jit(solution)/shard_map/all_to_all | solution.py:33
  (23 other events, 823.2 us)
